TPU v7x, 32 devices: a whole 2x2x4 slice. The times are simulated.
32 devices in a mesh: row: 8 (over y, x, core), col: 4 (over z).
Axes of the slice: x: 2, y: 2, z: 4, core: 2. Of those that a mesh axis runs over, the one named last changes fastest.
Arguments:
- features: bfloat16 [32768, 512], P('col', 'row'), may hold values from -6 to 6
- weight_t: bfloat16 [512, 512], P(None, 'row'), may hold values from -0.25 to 0.25
- tiles: bfloat16 [8192, 128, 128], P(('row', 'col')), may hold values from -0.15625 to 0.15625
- coords: int32 [2, 8192], P(None, ('row', 'col')), may hold values from 0 to 63, as said below
- counts: int32 [32], P(('row', 'col')), may hold values from 32 to 256, as said below
Outputs:
- output: bfloat16 [32768, 512], P('row', 'col')
Inputs may be any that keep to these rules, and one draw needn't show every extreme that they name: coords[0] of a slot lies in 0 to 31 and coords[1] in 0 to 63; the live slots of one grid cell name distinct tiles. `counts`: some grid cell has all 256 slots live in every draw.
All inputs are finite; a program needn't handle non-finite values.
Results may differ from a plain program's by a relative error of at most 0.0095.
Values may be sent and summed in bfloat16 or wider, within the bound.
A program may use at most 128 MiB of HBM per device.

v0:
```python
import jax
import jax.numpy as jnp
from jax import lax
from jax.sharding import PartitionSpec as P

TROW = 32


def tile_apply(tiles, rows, cols, count, source):
    maxt = tiles.shape[0]
    tile = tiles.shape[1]
    width = source.shape[2]
    tcol_here = source.shape[0]
    group = min(32, maxt)
    offsets = jnp.arange(group, dtype=jnp.int32)
    col_lanes = jnp.arange(tcol_here, dtype=jnp.int32)
    row_lanes = jnp.arange(TROW, dtype=jnp.int32)

    def step(index, total):
        start = (index * group).astype(jnp.int32)
        block = lax.dynamic_slice_in_dim(tiles, start, group, 0)
        block_rows = lax.dynamic_slice_in_dim(rows, start, group, 0)
        block_cols = lax.dynamic_slice_in_dim(cols, start, group, 0)
        live = start + offsets < count
        pick_cols = (block_cols[:, None] == col_lanes[None, :]).astype(jnp.bfloat16)
        inputs = jnp.einsum(
            "gc,cjw->gjw", pick_cols, source, preferred_element_type=jnp.float32
        ).astype(jnp.bfloat16)
        prod = jnp.einsum("gij,gjw->giw", block, inputs, preferred_element_type=jnp.float32)
        place_rows = ((block_rows[:, None] == row_lanes[None, :]) & live[:, None]).astype(
            jnp.float32
        )
        added = jnp.einsum("gt,giw->tiw", place_rows, prod, precision=lax.Precision.HIGHEST)
        return total + added

    turns = (count + group - 1) // group
    total = lax.fori_loop(0, turns, step, jnp.zeros((TROW, tile, width), jnp.float32))
    return total.reshape(TROW * tile, width)


def body(features, weight_t, tiles, coords, counts):
    rows = coords[0]
    cols = coords[1]
    count = counts[0]
    tile = tiles.shape[1]
    tcol_here = features.shape[0] // tile
    panel, weight_full = (
        lax.all_gather(features, "row", axis=1, tiled=True),
        lax.all_gather(weight_t, "row", axis=1, tiled=True),
    )
    spread = tile_apply(tiles, rows, cols, count, panel.reshape(tcol_here, tile, panel.shape[1]))
    partial_value = lax.dot_general(
        spread,
        weight_full.astype(jnp.float32),
        (((1,), (1,)), ((), ())),
        precision=lax.Precision.HIGHEST,
    )
    summed = lax.psum_scatter(partial_value, "col", scatter_dimension=1, tiled=True)
    return summed.astype(jnp.bfloat16)


def solution(mesh):
    placed = (
        P("col", "row"),
        P(None, "row"),
        P(("row", "col"), None, None),
        P(None, ("row", "col")),
        P(("row", "col")),
    )
    return jax.shard_map(
        body, mesh=mesh, in_specs=placed, out_specs=P("row", "col"), check_vma=False
    )
```

profile of v0, /device:TPU:0, one launch (start us, length us, event | category | flops | bytes accessed | tf_op | source)
XLA Modules:
  0.0 516.9 jit_solution(8024863803451204911)
XLA Ops:
  6.5 0.7 all-gather.2.cloned.1.call-update
  8.0 11.6 %all_gather.7 = bf16[512,512]{0,1:T(8,128)(2,1)S(1)} all-gather(bf16[512,64]{0,1:T(8,128)(2,1)} %param.8), channel_id=1, replica_groups=mesh['row'=8,'col'=4] {'row'}, dimensions={1}, use_global_device_ids=true | all-gather | bytes 589824 | tf_op jit(solution)/shard_map/all_gather | solution.py:49
  19.6 0.8 fusion.23
  20.4 45.9 %all-gather.2.cloned.1.call-done = bf16[8192,512]{0,1:T(8,128)(2,1)} async-done(((bf16[8192,64]{0,1:T(8,128)(2,1)}), bf16[8192,512]{0,1:T(8,128)(2,1)}) %all-gather.2.cloned.1.call-update) | async-done | bytes 8388624 | tf_op jit(solution)/shard_map/all_gather | solution.py:48
  66.2 12.0 %copy.7 = bf16[8192,512]{1,0:T(8,128)(2,1)} copy(bf16[8192,512]{0,1:T(8,128)(2,1)} %all-gather.2.cloned.1.call-done) | data formatting | bytes 16777216 | tf_op jit(solution)/shard_map/all_gather | solution.py:48
  78.2 4.3 broadcast_in_dim.13
  82.5 132.6 %while.13 = (s32[]{:T(128)}, f32[32,128,512]{2,0,1:T(8,128)}, s32[]{:T(128)}, s32[256]{0:T(256)S(1)}, s32[]{:T(128)}, /*index=5*/bf16[256,128,128]{2,1,0:T(8,128...) while((s32[]{:T(128)}, f32[32,128,512]{2,0,1:T(8,128)}, ...), condition=%wide.region_1.2_spmd.clone.clone, body=%wide.region_0.1_spmd.clone.clone.sunk | while | flops 1612713984 | bytes 51381240 | solution.py:37
  82.6 13.4 %fusion.41 = bf16[32,128,512]{2,0,1:T(8,128)(2,1)S(1)} fusion(bf16[64,128,512]{2,1,0:T(8,128)(2,1)} %get-tuple-element.233, s32[32]{0:T(128)S(1)} %dynamic_slice.24), kind=kOutput, calls=%fused_computation.5.clone.1 | convolution fusion | flops 268437504 | bytes 12583040 | tf_op jit(solution)/shard_map/while/body/gc,cjw->gjw/dot_general | solution.py:26
  96.0 6.4 %fusion.42 = f32[32,128,512]{2,1,0:T(8,128)S(1)} fusion(bf16[32,128,512]{2,0,1:T(8,128)(2,1)S(1)} %fusion.41, bf16[256,128,128]{2,1,0:T(8,128)(2,1)} %get-tuple-element.231, s32[]{:T(128)S(6)} %select_n.15), kind=kOutput, calls=%fused_computation.7.clone.1 | convolution fusion | flops 536870912 | bytes 13631492 | tf_op jit(solution)/shard_map/while/body/gij,gjw->giw/dot_general | solution.py:29
  102.3 0.1 dynamic_slice.25
  102.4 0.7 fusion.43
  103.1 12.6 %fusion.44 = f32[32,128,512]{2,0,1:T(8,128)} fusion(f32[32,128,512]{2,0,1:T(8,128)} %get-tuple-element.215, f32[32,128,512]{2,1,0:T(8,128)S(1)} %fusion.42, s32[32]{0:T(128)S(1)} %dynamic_slice.25, pred[32]{0:T(512)(128)(4,1)S(1)} %fusion.43), kind=kOutput, calls=%fused_computation.8.clone.1 | convolution fusion | flops 807405568 | bytes 25165984 | tf_op jit(solution)/shard_map/while/body/gt,giw->tiw/dot_general | solution.py:33
  115.7 0.1 dynamic_slice.24
  115.7 13.4 %fusion.41 = bf16[32,128,512]{2,0,1:T(8,128)(2,1)S(1)} fusion(bf16[64,128,512]{2,1,0:T(8,128)(2,1)} %get-tuple-element.233, s32[32]{0:T(128)S(1)} %dynamic_slice.24), kind=kOutput, calls=%fused_computation.5.clone.1 | convolution fusion | flops 268437504 | bytes 12583040 | tf_op jit(solution)/shard_map/while/body/gc,cjw->gjw/dot_general | solution.py:26
  129.1 6.4 %fusion.42 = f32[32,128,512]{2,1,0:T(8,128)S(1)} fusion(bf16[32,128,512]{2,0,1:T(8,128)(2,1)S(1)} %fusion.41, bf16[256,128,128]{2,1,0:T(8,128)(2,1)} %get-tuple-element.231, s32[]{:T(128)S(6)} %select_n.15), kind=kOutput, calls=%fused_computation.7.clone.1 | convolution fusion | flops 536870912 | bytes 13631492 | tf_op jit(solution)/shard_map/while/body/gij,gjw->giw/dot_general | solution.py:29
  135.5 0.1 dynamic_slice.25
  135.5 0.7 fusion.43
  136.2 12.6 %fusion.44 = f32[32,128,512]{2,0,1:T(8,128)} fusion(f32[32,128,512]{2,0,1:T(8,128)} %get-tuple-element.215, f32[32,128,512]{2,1,0:T(8,128)S(1)} %fusion.42, s32[32]{0:T(128)S(1)} %dynamic_slice.25, pred[32]{0:T(512)(128)(4,1)S(1)} %fusion.43), kind=kOutput, calls=%fused_computation.8.clone.1 | convolution fusion | flops 807405568 | bytes 25165984 | tf_op jit(solution)/shard_map/while/body/gt,giw->tiw/dot_general | solution.py:33
  148.9 13.4 %fusion.41 = bf16[32,128,512]{2,0,1:T(8,128)(2,1)S(1)} fusion(bf16[64,128,512]{2,1,0:T(8,128)(2,1)} %get-tuple-element.233, s32[32]{0:T(128)S(1)} %dynamic_slice.24), kind=kOutput, calls=%fused_computation.5.clone.1 | convolution fusion | flops 268437504 | bytes 12583040 | tf_op jit(solution)/shard_map/while/body/gc,cjw->gjw/dot_general | solution.py:26
  162.3 6.4 %fusion.42 = f32[32,128,512]{2,1,0:T(8,128)S(1)} fusion(bf16[32,128,512]{2,0,1:T(8,128)(2,1)S(1)} %fusion.41, bf16[256,128,128]{2,1,0:T(8,128)(2,1)} %get-tuple-element.231, s32[]{:T(128)S(6)} %select_n.15), kind=kOutput, calls=%fused_computation.7.clone.1 | convolution fusion | flops 536870912 | bytes 13631492 | tf_op jit(solution)/shard_map/while/body/gij,gjw->giw/dot_general | solution.py:29
  168.6 0.1 dynamic_slice.25
  168.7 0.7 fusion.43
  169.4 12.6 %fusion.44 = f32[32,128,512]{2,0,1:T(8,128)} fusion(f32[32,128,512]{2,0,1:T(8,128)} %get-tuple-element.215, f32[32,128,512]{2,1,0:T(8,128)S(1)} %fusion.42, s32[32]{0:T(128)S(1)} %dynamic_slice.25, pred[32]{0:T(512)(128)(4,1)S(1)} %fusion.43), kind=kOutput, calls=%fused_computation.8.clone.1 | convolution fusion | flops 807405568 | bytes 25165984 | tf_op jit(solution)/shard_map/while/body/gt,giw->tiw/dot_general | solution.py:33
  182.0 13.4 %fusion.41 = bf16[32,128,512]{2,0,1:T(8,128)(2,1)S(1)} fusion(bf16[64,128,512]{2,1,0:T(8,128)(2,1)} %get-tuple-element.233, s32[32]{0:T(128)S(1)} %dynamic_slice.24), kind=kOutput, calls=%fused_computation.5.clone.1 | convolution fusion | flops 268437504 | bytes 12583040 | tf_op jit(solution)/shard_map/while/body/gc,cjw->gjw/dot_general | solution.py:26
  195.4 6.4 %fusion.42 = f32[32,128,512]{2,1,0:T(8,128)S(1)} fusion(bf16[32,128,512]{2,0,1:T(8,128)(2,1)S(1)} %fusion.41, bf16[256,128,128]{2,1,0:T(8,128)(2,1)} %get-tuple-element.231, s32[]{:T(128)S(6)} %select_n.15), kind=kOutput, calls=%fused_computation.7.clone.1 | convolution fusion | flops 536870912 | bytes 13631492 | tf_op jit(solution)/shard_map/while/body/gij,gjw->giw/dot_general | solution.py:29
  201.8 0.1 dynamic_slice.25
  201.9 0.7 fusion.43
  202.5 12.6 %fusion.44 = f32[32,128,512]{2,0,1:T(8,128)} fusion(f32[32,128,512]{2,0,1:T(8,128)} %get-tuple-element.215, f32[32,128,512]{2,1,0:T(8,128)S(1)} %fusion.42, s32[32]{0:T(128)S(1)} %dynamic_slice.25, pred[32]{0:T(512)(128)(4,1)S(1)} %fusion.43), kind=kOutput, calls=%fused_computation.8.clone.1 | convolution fusion | flops 807405568 | bytes 25165984 | tf_op jit(solution)/shard_map/while/body/gt,giw->tiw/dot_general | solution.py:33
  215.1 8.2 %copy.8 = f32[32,128,512]{2,1,0:T(8,128)S(1)} copy(f32[32,128,512]{2,0,1:T(8,128)} %get-tuple-element.88) | data formatting | bytes 16777216 | tf_op jit(solution)/shard_map/while | solution.py:37
  223.4 8.9 %fusion.24 = f32[4096,512]{1,0:T(8,128)} fusion(f32[4096,512]{1,0:T(8,128)S(1)} %bitcast.19, bf16[512,512]{0,1:T(8,128)(2,1)S(1)} %all_gather.7), kind=kOutput, calls=%fused_computation.22 | convolution fusion | flops 12884901888 | bytes 17301504 | tf_op jit(solution)/shard_map/dot_general | solution.py:52
  232.3 275.1 %reduce-scatter.2.cloned.1.call-done = f32[4096,128]{1,0:T(8,128)} async-done(((f32[4096,512]{1,0:T(8,128)}), f32[4096,128]{1,0:T(8,128)}) %reduce-scatter.2.cloned.1.call-update) | async-done | bytes 2097168 | tf_op jit(solution)/shard_map/reduce_scatter | solution.py:58
  507.4 2.7 convert_element_type.12
  (6 shorter events, 0.3 us)
Async XLA Ops:
  6.5 59.7 %all-gather.2.cloned.1.call-start = ((), (), s32[]{:S(2)}) async-start(), calls=%async_computation.1 | async-start | bytes 9437184 | tf_op jit(solution)/shard_map/all_gather | solution.py:48
  7.3 500.1 %reduce-scatter.2.cloned.1.call-start = ((), (), s32[]{:S(2)}) async-start(), calls=%async_computation.2 | async-start | bytes 10485760 | tf_op jit(solution)/shard_map/reduce_scatter | solution.py:58
Sparse Core Ops, SparseCore 0:
  9.2 56.9 all-gather.1
  232.4 274.9 reduce-scatter.1
where the time goes:
time: 518 us; the launch traced here: 517 us
  waiting for transfers between devices  322 us (62%)
  matrix products  138 us (27%)
  local copies, waits for them, and re-layouts  25.9 us (5%)
  between operations  14.1 us (3%)
  blocking collectives  11.6 us (2%)
  other arithmetic  5.26 us (1%)
    reduce_scatter x1, waiting for transfers between devices, body(): lax.psum_scatter(partial_value, 'col', scatter_dimension=1, tiled=True)  275 us
    dot_general x4, matrix products, step(): jnp.einsum('gc,cjw->gjw', pick_cols, source, preferred_element_type=jnp.f...  53.5 us
    dot_general x4, matrix products, step(): jnp.einsum('gt,giw->tiw', place_rows, prod, precision=lax.Precision.HIGHEST)  50.4 us
    all_gather x1, waiting for transfers between devices, body(): lax.all_gather(features, 'row', axis=1, tiled=True)  45.9 us
    dot_general x4, matrix products, step(): jnp.einsum('gij,gjw->giw', block, inputs, preferred_element_type=jnp.floa...  25.4 us
    all_gather x1, local copies, waits for them, and re-layouts, body(): lax.all_gather(features, 'row', axis=1, tiled=True)  12 us
    all_gather x1, blocking collectives, body(): lax.all_gather(weight_t, 'row', axis=1, tiled=True)  11.6 us
  transfers between devices with their start and end apart: 2, of which 2 were waited for; matrix products, arithmetic and copies ran while one was open for 0% of the time, Pallas kernels for 0%

commit v1 on v0

--- a/solution.py
+++ b/solution.py
@@ -45,7 +45,7 @@
     tile = tiles.shape[1]
     tcol_here = features.shape[0] // tile
     panel, weight_full = (
-        lax.all_gather(features, "row", axis=1, tiled=True),
+        jnp.concatenate(lax.all_gather(features, "row"), axis=1),
         lax.all_gather(weight_t, "row", axis=1, tiled=True),
     )
     spread = tile_apply(tiles, rows, cols, count, panel.reshape(tcol_here, tile, panel.shape[1]))

time: 518 us -> 536 us (1.035)
  local copies, waits for them, and re-layouts: 25.9 us -> 43.5 us
    unnamed x0 -> x2, local copies, waits for them, and re-layouts: none -> 22 us
where the time goes in v1:
time: 536 us; the launch traced here: 535 us
  waiting for transfers between devices  322 us (60%)
  matrix products  138 us (26%)
  local copies, waits for them, and re-layouts  43.5 us (8%)
  between operations  14.1 us (3%)
  blocking collectives  11.6 us (2%)
    reduce_scatter x1, waiting for transfers between devices, body(): lax.psum_scatter(partial_value, 'col', scatter_dimension=1, tiled=True)  275 us
    dot_general x4, matrix products, step(): jnp.einsum('gc,cjw->gjw', pick_cols, source, preferred_element_type=jnp.f...  53.5 us
    dot_general x4, matrix products, step(): jnp.einsum('gt,giw->tiw', place_rows, prod, precision=lax.Precision.HIGHEST)  50.6 us
    all_gather x1, waiting for transfers between devices, body(): lax.all_gather(features, 'row')  45.9 us
    dot_general x4, matrix products, step(): jnp.einsum('gij,gjw->giw', block, inputs, preferred_element_type=jnp.floa...  25.4 us
    unnamed x2, local copies, waits for them, and re-layouts  22 us
    all_gather x1, blocking collectives, body(): lax.all_gather(weight_t, 'row', axis=1, tiled=True)  11.6 us
  transfers between devices with their start and end apart: 2, of which 2 were waited for; matrix products, arithmetic and copies ran while one was open for 0% of the time, Pallas kernels for 0%

profile of v1, /device:TPU:0, one launch (start us, length us, event | category | flops | bytes accessed | tf_op | source)
XLA Modules:
  0.0 534.9 jit_solution(13196409784644488448)
XLA Ops:
  6.5 0.7 all-gather.3.cloned.1.call-update
  8.0 11.6 %all_gather.11 = bf16[512,512]{0,1:T(8,128)(2,1)S(1)} all-gather(bf16[512,64]{0,1:T(8,128)(2,1)} %param.8), channel_id=1, replica_groups=mesh['row'=8,'col'=4] {'row'}, dimensions={1}, use_global_device_ids=true | all-gather | bytes 589824 | tf_op jit(solution)/shard_map/all_gather | solution.py:49
  19.6 0.8 fusion.23
  20.4 45.9 %all-gather.3.cloned.1.call-done = bf16[65536,64]{0,1:T(8,128)(2,1)} async-done(((bf16[8192,64]{0,1:T(8,128)(2,1)}), bf16[65536,64]{0,1:T(8,128)(2,1)}) %all-gather.3.cloned.1.call-update) | async-done | bytes 8388624 | tf_op jit(solution)/shard_map/all_gather | solution.py:48
  66.3 7.6 %copy.24 = bf16[8,8,8,8192]{3,2,0,1:T(8,128)(2,1)} copy(bf16[8,8,8,8192]{3,2,1,0:T(8,128)(2,1)} %bitcast.30) | data formatting | bytes 16777216 | tf_op jit(solution)/shard_map/all_gather | solution.py:48
  73.9 9.3 %copy.14 = bf16[64,8,64,128]{3,2,1,0:T(8,128)(2,1)} copy(bf16[64,8,64,128]{3,1,2,0:T(8,128)(2,1)} %bitcast.28) | data formatting | bytes 16777216
  83.2 12.7 %copy.8 = bf16[64,128,512]{2,1,0:T(8,128)(2,1)} copy(bf16[64,128,512]{1,0,2:T(8,128)(2,1)} %bitcast.29) | data formatting | bytes 16777216
  95.8 4.3 broadcast_in_dim.13
  100.1 132.8 %while.13 = (s32[]{:T(128)}, f32[32,128,512]{2,0,1:T(8,128)}, s32[]{:T(128)}, s32[256]{0:T(256)S(1)}, s32[]{:T(128)}, /*index=5*/bf16[256,128,128]{2,1,0:T(8,128...) while((s32[]{:T(128)}, f32[32,128,512]{2,0,1:T(8,128)}, ...), condition=%wide.region_1.2_spmd.clone.clone, body=%wide.region_0.1_spmd.clone.clone.sunk | while | flops 1612713984 | bytes 51381240 | solution.py:37
  100.2 13.4 %fusion.41 = bf16[32,128,512]{2,0,1:T(8,128)(2,1)S(1)} fusion(bf16[64,128,512]{2,1,0:T(8,128)(2,1)} %get-tuple-element.241, s32[32]{0:T(128)S(1)} %dynamic_slice.24), kind=kOutput, calls=%fused_computation.5.clone.1 | convolution fusion | flops 268437504 | bytes 12583040 | tf_op jit(solution)/shard_map/while/body/gc,cjw->gjw/dot_general | solution.py:26
  113.6 6.4 %fusion.42 = f32[32,128,512]{2,1,0:T(8,128)S(1)} fusion(bf16[32,128,512]{2,0,1:T(8,128)(2,1)S(1)} %fusion.41, bf16[256,128,128]{2,1,0:T(8,128)(2,1)} %get-tuple-element.239, s32[]{:T(128)S(6)} %select_n.15), kind=kOutput, calls=%fused_computation.7.clone.1 | convolution fusion | flops 536870912 | bytes 13631492 | tf_op jit(solution)/shard_map/while/body/gij,gjw->giw/dot_general | solution.py:29
  119.9 0.1 dynamic_slice.25
  120.0 0.7 fusion.43
  120.7 12.7 %fusion.44 = f32[32,128,512]{2,0,1:T(8,128)} fusion(f32[32,128,512]{2,0,1:T(8,128)} %get-tuple-element.223, f32[32,128,512]{2,1,0:T(8,128)S(1)} %fusion.42, s32[32]{0:T(128)S(1)} %dynamic_slice.25, pred[32]{0:T(512)(128)(4,1)S(1)} %fusion.43), kind=kOutput, calls=%fused_computation.8.clone.1 | convolution fusion | flops 807405568 | bytes 25165984 | tf_op jit(solution)/shard_map/while/body/gt,giw->tiw/dot_general | solution.py:33
  133.4 13.4 %fusion.41 = bf16[32,128,512]{2,0,1:T(8,128)(2,1)S(1)} fusion(bf16[64,128,512]{2,1,0:T(8,128)(2,1)} %get-tuple-element.241, s32[32]{0:T(128)S(1)} %dynamic_slice.24), kind=kOutput, calls=%fused_computation.5.clone.1 | convolution fusion | flops 268437504 | bytes 12583040 | tf_op jit(solution)/shard_map/while/body/gc,cjw->gjw/dot_general | solution.py:26
  146.8 6.4 %fusion.42 = f32[32,128,512]{2,1,0:T(8,128)S(1)} fusion(bf16[32,128,512]{2,0,1:T(8,128)(2,1)S(1)} %fusion.41, bf16[256,128,128]{2,1,0:T(8,128)(2,1)} %get-tuple-element.239, s32[]{:T(128)S(6)} %select_n.15), kind=kOutput, calls=%fused_computation.7.clone.1 | convolution fusion | flops 536870912 | bytes 13631492 | tf_op jit(solution)/shard_map/while/body/gij,gjw->giw/dot_general | solution.py:29
  153.1 0.1 dynamic_slice.25
  153.2 0.7 fusion.43
  153.9 12.7 %fusion.44 = f32[32,128,512]{2,0,1:T(8,128)} fusion(f32[32,128,512]{2,0,1:T(8,128)} %get-tuple-element.223, f32[32,128,512]{2,1,0:T(8,128)S(1)} %fusion.42, s32[32]{0:T(128)S(1)} %dynamic_slice.25, pred[32]{0:T(512)(128)(4,1)S(1)} %fusion.43), kind=kOutput, calls=%fused_computation.8.clone.1 | convolution fusion | flops 807405568 | bytes 25165984 | tf_op jit(solution)/shard_map/while/body/gt,giw->tiw/dot_general | solution.py:33
  166.6 13.4 %fusion.41 = bf16[32,128,512]{2,0,1:T(8,128)(2,1)S(1)} fusion(bf16[64,128,512]{2,1,0:T(8,128)(2,1)} %get-tuple-element.241, s32[32]{0:T(128)S(1)} %dynamic_slice.24), kind=kOutput, calls=%fused_computation.5.clone.1 | convolution fusion | flops 268437504 | bytes 12583040 | tf_op jit(solution)/shard_map/while/body/gc,cjw->gjw/dot_general | solution.py:26
  180.0 6.4 %fusion.42 = f32[32,128,512]{2,1,0:T(8,128)S(1)} fusion(bf16[32,128,512]{2,0,1:T(8,128)(2,1)S(1)} %fusion.41, bf16[256,128,128]{2,1,0:T(8,128)(2,1)} %get-tuple-element.239, s32[]{:T(128)S(6)} %select_n.15), kind=kOutput, calls=%fused_computation.7.clone.1 | convolution fusion | flops 536870912 | bytes 13631492 | tf_op jit(solution)/shard_map/while/body/gij,gjw->giw/dot_general | solution.py:29
  186.4 0.7 fusion.43
  187.1 12.7 %fusion.44 = f32[32,128,512]{2,0,1:T(8,128)} fusion(f32[32,128,512]{2,0,1:T(8,128)} %get-tuple-element.223, f32[32,128,512]{2,1,0:T(8,128)S(1)} %fusion.42, s32[32]{0:T(128)S(1)} %dynamic_slice.25, pred[32]{0:T(512)(128)(4,1)S(1)} %fusion.43), kind=kOutput, calls=%fused_computation.8.clone.1 | convolution fusion | flops 807405568 | bytes 25165984 | tf_op jit(solution)/shard_map/while/body/gt,giw->tiw/dot_general | solution.py:33
  199.8 13.4 %fusion.41 = bf16[32,128,512]{2,0,1:T(8,128)(2,1)S(1)} fusion(bf16[64,128,512]{2,1,0:T(8,128)(2,1)} %get-tuple-element.241, s32[32]{0:T(128)S(1)} %dynamic_slice.24), kind=kOutput, calls=%fused_computation.5.clone.1 | convolution fusion | flops 268437504 | bytes 12583040 | tf_op jit(solution)/shard_map/while/body/gc,cjw->gjw/dot_general | solution.py:26
  213.2 6.4 %fusion.42 = f32[32,128,512]{2,1,0:T(8,128)S(1)} fusion(bf16[32,128,512]{2,0,1:T(8,128)(2,1)S(1)} %fusion.41, bf16[256,128,128]{2,1,0:T(8,128)(2,1)} %get-tuple-element.239, s32[]{:T(128)S(6)} %select_n.15), kind=kOutput, calls=%fused_computation.7.clone.1 | convolution fusion | flops 536870912 | bytes 13631492 | tf_op jit(solution)/shard_map/while/body/gij,gjw->giw/dot_general | solution.py:29
  219.5 0.1 dynamic_slice.25
  219.6 0.7 fusion.43
  220.3 12.7 %fusion.44 = f32[32,128,512]{2,0,1:T(8,128)} fusion(f32[32,128,512]{2,0,1:T(8,128)} %get-tuple-element.223, f32[32,128,512]{2,1,0:T(8,128)S(1)} %fusion.42, s32[32]{0:T(128)S(1)} %dynamic_slice.25, pred[32]{0:T(512)(128)(4,1)S(1)} %fusion.43), kind=kOutput, calls=%fused_computation.8.clone.1 | convolution fusion | flops 807405568 | bytes 25165984 | tf_op jit(solution)/shard_map/while/body/gt,giw->tiw/dot_general | solution.py:33
  232.9 8.2 %copy.9 = f32[32,128,512]{2,1,0:T(8,128)S(1)} copy(f32[32,128,512]{2,0,1:T(8,128)} %get-tuple-element.88) | data formatting | bytes 16777216 | tf_op jit(solution)/shard_map/while | solution.py:37
  241.2 8.9 %fusion.24 = f32[4096,512]{1,0:T(8,128)} fusion(f32[4096,512]{1,0:T(8,128)S(1)} %bitcast.27, bf16[512,512]{0,1:T(8,128)(2,1)S(1)} %all_gather.11), kind=kOutput, calls=%fused_computation.23 | convolution fusion | flops 12884901888 | bytes 17301504 | tf_op jit(solution)/shard_map/dot_general | solution.py:52
  250.1 275.3 %reduce-scatter.2.cloned.1.call-done = f32[4096,128]{1,0:T(8,128)} async-done(((f32[4096,512]{1,0:T(8,128)}), f32[4096,128]{1,0:T(8,128)}) %reduce-scatter.2.cloned.1.call-update) | async-done | bytes 2097168 | tf_op jit(solution)/shard_map/reduce_scatter | solution.py:58
  525.4 2.7 convert_element_type.12
  (8 shorter events, 0.4 us)
Async XLA Ops:
  6.5 59.7 %all-gather.3.cloned.1.call-start = ((), (), s32[]{:S(2)}) async-start(), calls=%async_computation.2 | async-start | bytes 9437184 | tf_op jit(solution)/shard_map/all_gather | solution.py:48
  7.3 518.1 %reduce-scatter.2.cloned.1.call-start = ((), (), s32[]{:S(2)}) async-start(), calls=%async_computation.1 | async-start | bytes 10485760 | tf_op jit(solution)/shard_map/reduce_scatter | solution.py:58
Sparse Core Ops, SparseCore 0:
  9.2 56.9 all-gather.2
  250.2 275.1 reduce-scatter.1
